TPU v7x, 32 devices: a whole 2x2x4 slice. The times are simulated.
32 devices in a mesh: member: 4 (over y, core), space: 8 (over z, x).
Axes of the slice: x: 2, y: 2, z: 4, core: 2. Of those that a mesh axis runs over, the one named last changes fastest.
Arguments:
- state: float32 [256, 128, 1024], P('member', 'space'), may hold values from -8 to 8
- obs_index: int32 [8192], P('space'), may hold values from 0 to 16383
- obs_value: float32 [8192], P('space'), may hold values from -6 to 6
- obs_scale: float32 [8192], P('space'), may hold values from 0.3 to 3
- ksat: float32 [128, 1024], P('space'), may hold values from 0.05 to 0.2
- storage: float32 [128, 1024], P('space'), may hold values from 0.5 to 4
- recharge: float32 [128, 1024], P('space'), may hold values from -1.8 to 1.8
- newton_counts: int32 [256], replicated, may hold values from 1 to 8, as said below
Outputs:
- forecast: float32 [256, 128, 1024], P('member', 'space')
Inputs may be any that keep to these rules, and one draw needn't show every extreme that they name: `newton_counts`: A count of 8 occurs in every draw.
All inputs are finite; a program needn't handle non-finite values.
Results may differ from a plain program's by a relative error of at most 0.0003.
Values sent between devices are 32-bit elements; how exact they have to be, the bound alone decides.
A program may use at most 64 MiB of HBM per device.

v0:
```python
import jax
import jax.numpy as jnp
from jax import lax
from jax.sharding import PartitionSpec as P

KMAX = 8
NS_ITERS = 12
HIGHEST_PRECISION = lax.Precision.HIGHEST
DAMPING = 0.3


def padded_2(array, sides, width):
    for axis, dim in sides:
        peers, length = (lax.axis_size(axis), array.shape[dim])
        up = [(i, (i + 1) % peers) for i in range(peers - 1)]
        down = [(j, i) for i, j in up]
        last = lax.slice_in_dim(array, length - width, length, axis=dim)
        leading = lax.slice_in_dim(array, 0, width, axis=dim)
        before = lax.ppermute(last, axis, up)
        after = lax.ppermute(leading, axis, down)
        array = jnp.concatenate([before, array, after], axis=dim)
    return array


def inverse_root(gram_matrix):
    order_size = gram_matrix.shape[0]
    identity = jnp.eye(order_size, dtype=jnp.float32)
    whole = identity + gram_matrix
    norm_value = jnp.sqrt(jnp.sum(whole * whole))
    upper_iter = whole / norm_value
    lower_iter = identity
    for sweep_index in range(NS_ITERS):
        middle = 1.5 * identity - 0.5 * jnp.dot(lower_iter, upper_iter, precision=HIGHEST_PRECISION)
        upper_iter = jnp.dot(upper_iter, middle, precision=HIGHEST_PRECISION)
        lower_iter = jnp.dot(middle, lower_iter, precision=HIGHEST_PRECISION)
    return lower_iter / jnp.sqrt(norm_value)


def face_flux(padded, conduct):
    wide_level = jnp.pad(padded, ((0, 0), (0, 0), (1, 1)))
    wide_cond = jnp.pad(conduct, ((0, 0), (0, 0), (1, 1)))
    centre_level = wide_level[:, 1:-1, 1:-1]
    centre_cond = wide_cond[:, 1:-1, 1:-1]
    height = centre_level.shape[1]
    breadth = centre_level.shape[2]
    divergence = jnp.zeros_like(centre_level)
    for offset_row, offset_col in ((0, 1), (2, 1), (1, 0), (1, 2)):
        other_level = wide_level[
            :, offset_row : offset_row + height, offset_col : offset_col + breadth
        ]
        other_cond = wide_cond[
            :, offset_row : offset_row + height, offset_col : offset_col + breadth
        ]
        divergence = divergence + 0.5 * (centre_cond + other_cond) * (other_level - centre_level)
    return divergence


def sweep_group(start_iter, goal, storage, group_counts):

    def sweep_once(sweep_index, iterate):
        bend_value = jnp.tanh(iterate)
        derivative = 1.0 + storage * (1.0 - bend_value * bend_value)
        stepped = iterate - DAMPING * (iterate + storage * bend_value - goal) / derivative
        return jnp.where((group_counts > sweep_index)[:, None, None], stepped, iterate)

    return lax.fori_loop(0, jnp.max(group_counts), sweep_once, start_iter)


def relax(pressure, drive_term, storage, counts):
    target = pressure + storage * jnp.tanh(pressure) + drive_term
    pieces = []
    for first_member in range(0, pressure.shape[0], 8):
        pieces.append(
            sweep_group(
                pressure[first_member : first_member + 8],
                target[first_member : first_member + 8],
                storage,
                counts[first_member : first_member + 8],
            )
        )
    return jnp.concatenate(pieces, axis=0)


def advance(padded, padded_ksat, storage, recharge, counts):
    conduct = padded_ksat * jax.nn.sigmoid(padded)
    drive_term = face_flux(padded, conduct) + recharge
    return relax(padded[:, 1:-1], drive_term, storage, counts)


def on_device(state, obs_index, obs_value, obs_scale, ksat, storage, recharge, newton_counts):
    local_members, tile_rows, tile_width = state.shape
    groups = lax.axis_size("member")
    members = local_members * groups
    tile_cells = tile_rows * tile_width
    block_cells = tile_cells // groups
    share = local_members // groups
    position = lax.axis_index("member")
    regrouped = lax.all_to_all(
        state.reshape(local_members, tile_cells), "member", split_axis=1, concat_axis=0, tiled=True
    )
    mean_state = jnp.mean(regrouped, axis=0)
    anomaly = regrouped - mean_state
    local_cell = obs_index - position * block_cells
    inside = (local_cell >= 0) & (local_cell < block_cells)
    picked = jnp.clip(local_cell, 0, block_cells - 1)
    weight = jnp.where(inside, obs_scale, 0.0)
    root_count = jnp.sqrt(jnp.float32(members - 1))
    spread = jnp.take(anomaly, picked, axis=1) * weight / root_count
    innovation = weight * (obs_value - jnp.take(mean_state, picked))
    gram_part = jnp.dot(spread, spread.T, precision=HIGHEST_PRECISION)
    drive_part = jnp.dot(spread, innovation, precision=HIGHEST_PRECISION)
    gram_matrix, drive_vector = lax.psum((gram_part, drive_part), ("member", "space"))
    root_inverse = inverse_root(gram_matrix)
    mean_weights = jnp.dot(
        root_inverse,
        jnp.dot(root_inverse, drive_vector, precision=HIGHEST_PRECISION),
        precision=HIGHEST_PRECISION,
    )
    transform = mean_weights[:, None] / root_count + root_inverse
    sequence = jnp.arange(members, dtype=jnp.int32)
    owner_of = sequence // local_members
    sort_key = owner_of * ((KMAX + 1) * members) + (KMAX - newton_counts) * members + sequence
    ranking = jnp.argsort(sort_key)
    member_ids = ranking.reshape(groups, share, groups).transpose(2, 0, 1).reshape(members)
    transform = jnp.take(transform, member_ids, axis=1)
    own_ids = lax.dynamic_slice_in_dim(member_ids, position * local_members, local_members)
    own_counts = jnp.take(newton_counts, own_ids)
    analysis = mean_state + jnp.dot(transform.T, anomaly, precision=HIGHEST_PRECISION)
    owned = lax.all_to_all(analysis, "member", split_axis=0, concat_axis=1, tiled=True)
    pressure = owned.reshape(local_members, tile_rows, tile_width)
    stacked = jnp.concatenate([pressure, ksat[None]], axis=0)
    widened = padded_2(stacked, (("space", 1),), 1)
    ksat_wide = widened[local_members]
    pressure = advance(widened[:local_members], ksat_wide, storage, recharge, own_counts)
    widened = padded_2(pressure, (("space", 1),), 1)
    pressure = advance(widened, ksat_wide, storage, recharge, own_counts)
    final_field = pressure.reshape(local_members, tile_cells)
    arrived = lax.all_to_all(final_field, "member", split_axis=0, concat_axis=0, tiled=True)
    by_owner = member_ids.reshape(groups, groups, share)
    arrived_ids = (
        jnp.take(by_owner, position, axis=1).reshape(local_members) - position * local_members
    )
    final_field = jnp.take(arrived, jnp.argsort(arrived_ids), axis=0)
    return final_field.reshape(local_members, tile_rows, tile_width)


def solution(mesh):
    return jax.shard_map(
        on_device,
        mesh=mesh,
        in_specs=(
            P("member", "space", None),
            P("space"),
            P("space"),
            P("space"),
            P("space", None),
            P("space", None),
            P("space", None),
            P(),
        ),
        out_specs=P("member", "space", None),
        check_vma=False,
    )
```

profile of v0, /device:TPU:8, one launch (start us, length us, event | category | flops | bytes accessed | tf_op | source)
XLA Modules:
  0.0 656.5 jit_solution(13870586919959672134)
XLA Ops:
  12.4 6.6 %copy.22 = f32[64,4,4096]{2,0,1:T(8,128)} copy(f32[64,4,4096]{2,1,0:T(4,128)} %all_to_all.34) | data formatting | bytes 8388608 | tf_op jit(solution)/shard_map/all_to_all | solution.py:98
  27.6 44.5 %all-to-all-done = f32[64,4,4096]{2,0,1:T(8,128)} async-done(((f32[64,4,4096]{2,0,1:T(8,128)}), f32[64,4,4096]{2,0,1:T(8,128)}, u32[]{:S(2)}, u32[]{:S(2)}) %all-to-all-start) | async-done | bytes 4194336 | tf_op jit(solution)/shard_map/all_to_all | solution.py:98
  100.8 39.6 %psum.15 = f32[256]{0:T(256)S(1)} all-reduce(f32[256]{0:T(256)S(1)} %bitcast.112), channel_id=1, replica_groups=mesh['member'=4,'space'=8] {'member','space'}, use_global_device_ids=true, to_apply=%region_5.6 | all-reduce | flops 256 | bytes 2048 | tf_op jit(solution)/shard_map/psum | solution.py:112
  140.4 86.6 %all-reduce.6.cloned.1.call-done = f32[256,256]{1,0:T(8,128)} async-done(((f32[256,256]{1,0:T(8,128)}), f32[256,256]{1,0:T(8,128)}) %all-reduce.6.cloned.1.call-update) | async-done | bytes 262160 | tf_op jit(solution)/shard_map/psum | solution.py:112
  247.0 8.2 %convolution_add_fusion = f32[256,4096]{1,0:T(8,128)} fusion(f32[256,4096]{1,0:T(8,128)} %bitcast_subtract_fusion, f32[4096]{0:T(1024)S(1)} %broadcast_multiply_fusion, f32[256,256]{1,0:T(8,128)S(1)} %gather_fusion.2, pred[256]{0:T(512)(128)(4,1)S(1)} %compare_and_fusion.1), kind=kOutput, calls=%fused_computation.51 | convolution fusion | flops 3222339584 | bytes 8667392 | tf_op jit(solution)/shard_map/dot_general | solution.py:128
  262.5 45.8 %all-to-all-done.1 = f32[4,64,4096]{2,1,0:T(8,128)} async-done(((f32[4,64,4096]{2,1,0:T(8,128)}), f32[4,64,4096]{2,1,0:T(8,128)}, u32[]{:S(2)}, u32[]{:S(2)}) %all-to-all-start.1) | async-done | bytes 4194336 | tf_op jit(solution)/shard_map/all_to_all | solution.py:129
  308.3 6.9 %copy.28 = f32[64,4,4096]{2,1,0:T(4,128)} copy(f32[64,4,4096]{2,0,1:T(8,128)} %bitcast.13) | data formatting | bytes 8388608 | tf_op jit(solution)/shard_map/all_to_all | solution.py:129
  363.1 15.7 %fusion.6 = f32[64,16,1024]{2,1,0:T(8,128)} fusion(f32[64,18,1024]{2,1,0:T(8,128)S(1)} %get-tuple-element.768, f32[64,16,1024]{2,1,0:T(8,128)S(1)} %copy-done.2, f32[64,18,1024]{2,1,0:T(8,128)S(1)} %get-tuple-element.767, f32[65,1,1024]{2,1,0:T(1,128)} %collective-permute-done.1, f32[1,16,1024]{2,1,0:T(8,128)S(1)} %bitcast.106, ...), kind=kLoop, calls=%fused_computation.58 | loop fusion | flops 28311552 | bytes 34283520 | tf_op jit(solution)/shard_map/add | solution.py:70
  382.9 6.3 while.168
  389.3 9.4 %while.167 = (s32[]{:T(128)}, f32[8,16,1024]{2,1,0:T(8,128)}, s32[]{:T(128)}, s32[8]{0:T(128)S(1)}, f32[16,1024]{1,0:T(8,128)S(1)}, /*index=5*/f32[8,16,1024]{2,1,0:T(8,128)}, s32[]{:T(128)}) while((s32[]{:T(128)}, f32[8,16,1024]{2,1,0:T(8,128)}, s32[]{:T(128)}, s32[8]{0:T(128)S(1)}, f32[16,1024]{1,0:T(8,128)S(1)}, ...), condition=%wide.region_26.27_spmd, body=%wide.region_25.26_spmd.sunk | while | flops 1441802 | bytes 1638537 | solution.py:66
  403.6 6.9 %while.165 = (s32[]{:T(128)}, f32[8,16,1024]{2,1,0:T(8,128)S(1)}, s32[]{:T(128)}, s32[8]{0:T(128)S(1)}, f32[16,1024]{1,0:T(8,128)S(1)}, /*index=5*/f32[8,16,1024]{2,1,0:T(8,128)}, s32[]{:T(128)}) while((s32[]{:T(128)}, f32[8,16,1024]{2,1,0:T(8,128)S(1)}, s32[]{:T(128)}, s32[8]{0:T(128)S(1)}, f32[16,1024]{1,0:T(8,128)S(1)}, ...), condition=%wide.region_20.21_spmd, body=%wide.region_19.20_spmd.sunk | while | flops 1441802 | bytes 1638537 | solution.py:66
  410.5 7.2 %while.164 = (s32[]{:T(128)}, f32[8,16,1024]{2,1,0:T(8,128)S(1)}, s32[]{:T(128)}, s32[8]{0:T(128)S(1)}, f32[16,1024]{1,0:T(8,128)S(1)}, /*index=5*/f32[8,16,1024]{2,1,0:T(8,128)}, s32[]{:T(128)}) while((s32[]{:T(128)}, f32[8,16,1024]{2,1,0:T(8,128)S(1)}, s32[]{:T(128)}, s32[8]{0:T(128)S(1)}, f32[16,1024]{1,0:T(8,128)S(1)}, ...), condition=%wide.region_17.18_spmd, body=%wide.region_16.17_spmd.sunk | while | flops 1441802 | bytes 1638537 | solution.py:66
  417.7 16.9 %while.163 = (s32[]{:T(128)}, f32[8,16,1024]{2,1,0:T(8,128)S(1)}, s32[]{:T(128)}, s32[8]{0:T(128)S(1)}, f32[16,1024]{1,0:T(8,128)S(1)}, /*index=5*/f32[8,16,1024]{2,1,0:T(8,128)}, s32[]{:T(128)}) while((s32[]{:T(128)}, f32[8,16,1024]{2,1,0:T(8,128)S(1)}, s32[]{:T(128)}, s32[8]{0:T(128)S(1)}, f32[16,1024]{1,0:T(8,128)S(1)}, ...), condition=%wide.region_14.15_spmd, body=%wide.region_13.14_spmd.sunk | while | flops 1441802 | bytes 1638537 | solution.py:66
  439.1 17.4 %while.161 = (s32[]{:T(128)}, f32[8,16,1024]{2,1,0:T(8,128)S(1)}, s32[]{:T(128)}, s32[8]{0:T(128)S(1)}, f32[16,1024]{1,0:T(8,128)S(1)}, /*index=5*/f32[8,16,1024]{2,1,0:T(8,128)}, s32[]{:T(128)}) while((s32[]{:T(128)}, f32[8,16,1024]{2,1,0:T(8,128)S(1)}, s32[]{:T(128)}, s32[8]{0:T(128)S(1)}, f32[16,1024]{1,0:T(8,128)S(1)}, ...), condition=%wide.region_8.9_spmd, body=%wide.region_7.8_spmd.sunk | while | flops 1441802 | bytes 1638537 | solution.py:66
  467.9 6.3 collective-permute-done.2
  480.9 11.3 %fusion.18 = f32[64,16,1024]{2,1,0:T(8,128)} fusion(f32[64,18,1024]{2,1,0:T(8,128)S(1)} %get-tuple-element.770, f32[64,16,1024]{2,1,0:T(8,128)S(1)} %copy-done.8, f32[64,18,1024]{2,1,0:T(8,128)S(1)} %get-tuple-element.769, f32[64,1,1024]{2,1,0:T(1,128)} %collective-permute-done.3, f32[64,1,1024]{2,1,0:T(1,128)S(1)} %collective-permute-done.2, ...), kind=kLoop, calls=%fused_computation.70 | loop fusion | flops 26214400 | bytes 34209792 | tf_op jit(solution)/shard_map/add | solution.py:70
  496.3 6.3 while.176
  502.7 9.4 %while.175 = (s32[]{:T(128)}, f32[8,16,1024]{2,1,0:T(8,128)}, s32[]{:T(128)}, s32[8]{0:T(128)S(1)}, f32[16,1024]{1,0:T(8,128)S(1)}, /*index=5*/f32[8,16,1024]{2,1,0:T(8,128)}, s32[]{:T(128)}) while((s32[]{:T(128)}, f32[8,16,1024]{2,1,0:T(8,128)}, s32[]{:T(128)}, s32[8]{0:T(128)S(1)}, f32[16,1024]{1,0:T(8,128)S(1)}, ...), condition=%wide.region_43.44_spmd, body=%wide.region_42.43_spmd.sunk | while | flops 1441802 | bytes 1638537 | solution.py:66
  517.0 6.6 %while.173 = (s32[]{:T(128)}, f32[8,16,1024]{2,1,0:T(8,128)S(1)}, s32[]{:T(128)}, s32[8]{0:T(128)S(1)}, f32[16,1024]{1,0:T(8,128)S(1)}, /*index=5*/f32[8,16,1024]{2,1,0:T(8,128)}, s32[]{:T(128)}) while((s32[]{:T(128)}, f32[8,16,1024]{2,1,0:T(8,128)S(1)}, s32[]{:T(128)}, s32[8]{0:T(128)S(1)}, f32[16,1024]{1,0:T(8,128)S(1)}, ...), condition=%wide.region_39.40_spmd, body=%wide.region_38.39_spmd.sunk | while | flops 1441802 | bytes 1638537 | solution.py:66
  523.6 7.2 %while.172 = (s32[]{:T(128)}, f32[8,16,1024]{2,1,0:T(8,128)S(1)}, s32[]{:T(128)}, s32[8]{0:T(128)S(1)}, f32[16,1024]{1,0:T(8,128)S(1)}, /*index=5*/f32[8,16,1024]{2,1,0:T(8,128)}, s32[]{:T(128)}) while((s32[]{:T(128)}, f32[8,16,1024]{2,1,0:T(8,128)S(1)}, s32[]{:T(128)}, s32[8]{0:T(128)S(1)}, f32[16,1024]{1,0:T(8,128)S(1)}, ...), condition=%wide.region_37.38_spmd, body=%wide.region_36.37_spmd.sunk | while | flops 1441802 | bytes 1638537 | solution.py:66
  530.8 16.9 %while.171 = (s32[]{:T(128)}, f32[8,16,1024]{2,1,0:T(8,128)S(1)}, s32[]{:T(128)}, s32[8]{0:T(128)S(1)}, f32[16,1024]{1,0:T(8,128)S(1)}, /*index=5*/f32[8,16,1024]{2,1,0:T(8,128)}, s32[]{:T(128)}) while((s32[]{:T(128)}, f32[8,16,1024]{2,1,0:T(8,128)S(1)}, s32[]{:T(128)}, s32[8]{0:T(128)S(1)}, f32[16,1024]{1,0:T(8,128)S(1)}, ...), condition=%wide.region_35.36_spmd, body=%wide.region_34.35_spmd.sunk | while | flops 1441802 | bytes 1638537 | solution.py:66
  552.3 17.4 %while.169 = (s32[]{:T(128)}, f32[8,16,1024]{2,1,0:T(8,128)S(1)}, s32[]{:T(128)}, s32[8]{0:T(128)S(1)}, f32[16,1024]{1,0:T(8,128)S(1)}, /*index=5*/f32[8,16,1024]{2,1,0:T(8,128)}, s32[]{:T(128)}) while((s32[]{:T(128)}, f32[8,16,1024]{2,1,0:T(8,128)S(1)}, s32[]{:T(128)}, s32[8]{0:T(128)S(1)}, f32[16,1024]{1,0:T(8,128)S(1)}, ...), condition=%wide.region_31.32_spmd, body=%wide.region_30.31_spmd.sunk | while | flops 1441802 | bytes 1638537 | solution.py:66
  589.3 45.2 %all-to-all-done.2 = f32[4,16,16384]{2,1,0:T(8,128)} async-done(((f32[4,16,16384]{2,1,0:T(8,128)}), f32[4,16,16384]{2,1,0:T(8,128)}, u32[]{:S(2)}, u32[]{:S(2)}) %all-to-all-start.2) | async-done | bytes 4194336 | tf_op jit(solution)/shard_map/all_to_all | solution.py:138
  634.6 7.7 %gather_fusion.4 = f32[64,16384]{1,0:T(8,128)} fusion(f32[64,16384]{1,0:T(8,128)} %bitcast.16, s32[1024]{0:T(1024)S(1)} %pad_clamp_fusion), kind=kCustom, calls=%fused_computation.4 | custom fusion | bytes 8388864 | tf_op jit(solution)/shard_map/jit(_take)/gather | solution.py:143
  (303 shorter events, 286.2 us)
Async XLA Ops:
  19.0 5.0 copy-start.1
  19.0 8.6 %copy-start.14 = (s32[1024]{0:T(1024)S(1)}, s32[1024]{0:T(1024)}, u32[]{:S(2)}) copy-start(s32[1024]{0:T(1024)} %param.41) | copy-start | bytes 12292
  19.0 53.2 %all-to-all-start = ((f32[64,4,4096]{2,0,1:T(8,128)}), f32[64,4,4096]{2,0,1:T(8,128)}, u32[]{:S(2)}, u32[]{:S(2)}) async-start(f32[64,4,4096]{2,0,1:T(8,128)} %copy.22), calls=%async_computation | async-start | bytes 8388608 | tf_op jit(solution)/shard_map/all_to_all | solution.py:98
  23.9 203.0 %all-reduce.6.cloned.1.call-start = ((), (), s32[]{:S(2)}) async-start(), calls=%async_computation.3 | async-start | bytes 524288 | tf_op jit(solution)/shard_map/psum | solution.py:112
  27.3 44.8 %copy-start.13 = (s32[4,16,4]{2,1,0:T(8,128)}, s32[4,16,4]{2,1,0:T(8,128)S(1)}, u32[]{:S(2)}) copy-start(s32[4,16,4]{2,1,0:T(8,128)S(1)} %reshape.168) | copy-start | bytes 3076
  91.1 5.7 copy-start.15
  91.1 5.7 copy-start.16
  255.2 53.0 %all-to-all-start.1 = ((f32[4,64,4096]{2,1,0:T(8,128)}), f32[4,64,4096]{2,1,0:T(8,128)}, u32[]{:S(2)}, u32[]{:S(2)}) async-start(f32[4,64,4096]{2,1,0:T(8,128)} %bitcast.102), calls=%async_computation.1 | async-start | bytes 8388608 | tf_op jit(solution)/shard_map/all_to_all | solution.py:129
  315.2 5.8 copy-start.9
  324.6 32.5 %collective-permute-start = (f32[65,1,1024]{2,1,0:T(1,128)}, f32[65,1,1024]{2,1,0:T(1,128)S(1)}, u32[]{:S(2)}, u32[]{:S(2)}) collective-permute-start(f32[65,1,1024]{2,1,0:T(1,128)} %get-tuple-element.771), channel_id=1, source_target_pairs={{0,1},{1,2},{2,3},{3,4},{4,5},{5,6},{6,7},{8,9},{9,10},{10,11},{11... | collective-permute-start | bytes 798728 | tf_op jit(solution)/shard_map/ppermute | solution.py:19
  328.0 29.1 %collective-permute-start.1 = (f32[65,1,1024]{2,1,0:T(1,128)}, f32[65,1,1024]{2,1,0:T(1,128)}, u32[]{:S(2)}, u32[]{:S(2)}) collective-permute-start(f32[65,1,1024]{2,1,0:T(1,128)} %get-tuple-element.772), channel_id=1, source_target_pairs={{1,0},{2,1},{3,2},{4,3},{5,4},{6,5},{7,6},{9,8},{10,9},{11,10},{12... | collective-permute-start | bytes 798728 | tf_op jit(solution)/shard_map/ppermute | solution.py:20
  359.2 3.8 copy-start.11
  378.8 4.1 copy-start.21
  382.9 6.4 copy-start.20
  389.2 9.4 %copy-start.19 = (s32[8]{0:T(128)S(1)}, s32[8]{0:T(128)}, u32[]{:S(2)}) copy-start(s32[8]{0:T(128)} %get-tuple-element.1693) | copy-start | bytes 100
  398.6 5.0 copy-start.18
  403.6 6.9 %copy-start.17 = (s32[8]{0:T(128)S(1)}, s32[8]{0:T(128)}, u32[]{:S(2)}) copy-start(s32[8]{0:T(128)} %get-tuple-element.1651) | copy-start | bytes 100
  461.1 13.1 %collective-permute-start.2 = (f32[64,1,1024]{2,1,0:T(1,128)}, f32[64,1,1024]{2,1,0:T(1,128)S(1)}, u32[]{:S(2)}, u32[]{:S(2)}) collective-permute-start(f32[64,1,1024]{2,1,0:T(1,128)} %get-tuple-element.781), channel_id=1, source_target_pairs={{0,1},{1,2},{2,3},{3,4},{4,5},{5,6},{6,7},{8,9},{9,10},{10,11},{11... | collective-permute-start | bytes 786440 | tf_op jit(solution)/shard_map/ppermute | solution.py:19
  463.6 13.4 %collective-permute-start.3 = (f32[64,1,1024]{2,1,0:T(1,128)}, f32[64,1,1024]{2,1,0:T(1,128)}, u32[]{:S(2)}, u32[]{:S(2)}) collective-permute-start(f32[64,1,1024]{2,1,0:T(1,128)} %get-tuple-element.782), channel_id=1, source_target_pairs={{1,0},{2,1},{3,2},{4,3},{5,4},{6,5},{7,6},{9,8},{10,9},{11,10},{12... | collective-permute-start | bytes 786440 | tf_op jit(solution)/shard_map/ppermute | solution.py:20
  467.9 13.0 %copy-start.8 = (f32[64,16,1024]{2,1,0:T(8,128)S(1)}, f32[64,16,1024]{2,1,0:T(8,128)}, u32[]{:S(2)}) copy-start(f32[64,16,1024]{2,1,0:T(8,128)} %copy-done.7) | copy-start | bytes 12582916
  467.9 13.0 %copy-start.12 = (f32[16,1024]{1,0:T(8,128)S(1)}, f32[16,1024]{1,0:T(8,128)}, u32[]{:S(2)}) copy-start(f32[16,1024]{1,0:T(8,128)} %param.46) | copy-start | bytes 196612
  569.7 5.0 copy-start.4
  569.7 5.8 copy-start.6
  581.3 53.3 %all-to-all-start.2 = ((f32[4,16,16384]{2,1,0:T(8,128)}), f32[4,16,16384]{2,1,0:T(8,128)}, u32[]{:S(2)}, u32[]{:S(2)}) async-start(f32[4,16,16384]{2,1,0:T(8,128)} %all_to_all.41), calls=%async_computation.2 | async-start | bytes 8388608 | tf_op jit(solution)/shard_map/all_to_all | solution.py:138
  (6 other events, 14.0 us)
Sparse Core Ops, SparseCore 0:
  100.1 126.7 all-reduce.5
where the time goes:
time: 669 us; the launch traced here: 656 us
  waiting for transfers between devices  231 us (35%)
  other arithmetic  155 us (23%)
  local copies, waits for them, and re-layouts  109 us (16%)
  loops' own time  49.4 us (7%)
  blocking collectives  39.6 us (6%)
  starting transfers between devices  28.5 us (4%)
  matrix products  28.2 us (4%)
  between operations  15.5 us (2%)
    select_n x62, other arithmetic, sweep_once(): jnp.where((group_counts > sweep_index)[:, None, None], stepped, iterate)  97 us
    psum x1, waiting for transfers between devices, on_device(): lax.psum((gram_part, drive_part), ('member', 'space'))  86.6 us
    another operation x16, loops' own time, sweep_group(): return lax.fori_loop(0, jnp.max(group_counts), sweep_once, start_iter)  49.4 us
    all_to_all x1, waiting for transfers between devices, on_device(): lax.all_to_all(analysis, 'member', split_axis=0, concat_axis=1, tiled=True)  45.8 us
    all_to_all x1, waiting for transfers between devices, on_device(): lax.all_to_all(final_field, 'member', split_axis=0, concat_axis=0, tiled=...  45.2 us
    all_to_all x1, waiting for transfers between devices, on_device(): lax.all_to_all(state.reshape(local_members, tile_cells), 'member', split_...  44.5 us
    psum x1, blocking collectives, on_device(): lax.psum((gram_part, drive_part), ('member', 'space'))  39.6 us
    add x2, other arithmetic, relax(): target = pressure + storage * jnp.tanh(pressure) + drive_term  27 us
  transfers between devices with their start and end apart: 8, of which 6 were waited for; matrix products, arithmetic and copies ran while one was open for 5% of the time, Pallas kernels for 0%

commit v1 on v0

--- a/solution.py
+++ b/solution.py
@@ -126,7 +126,12 @@
     own_ids = lax.dynamic_slice_in_dim(member_ids, position * local_members, local_members)
     own_counts = jnp.take(newton_counts, own_ids)
     analysis = mean_state + jnp.dot(transform.T, anomaly, precision=HIGHEST_PRECISION)
-    owned = lax.all_to_all(analysis, "member", split_axis=0, concat_axis=1, tiled=True)
+    owned = jnp.concatenate(
+        lax.all_to_all(
+            jnp.stack(jnp.split(analysis, lax.axis_size("member"), axis=0)), "member", 0, 0
+        ),
+        axis=1,
+    )
     pressure = owned.reshape(local_members, tile_rows, tile_width)
     stacked = jnp.concatenate([pressure, ksat[None]], axis=0)
     widened = padded_2(stacked, (("space", 1),), 1)

time: 669 us -> 667 us (level)
    all_to_all x1 -> x0, local copies, waits for them, and re-layouts: 6.9 us -> none  [on_device(): lax.all_to_all(analysis, 'member', split_axis=0, concat_axis=1, tiled=True)]
    unnamed x59 -> x73, local copies, waits for them, and re-layouts: 14.9 us -> 15.1 us
where the time goes in v1:
time: 667 us; the launch traced here: 655 us
  waiting for transfers between devices  231 us (35%)
  other arithmetic  159 us (24%)
  local copies, waits for them, and re-layouts  105 us (16%)
  loops' own time  50.2 us (8%)
  blocking collectives  39.6 us (6%)
  starting transfers between devices  28.6 us (4%)
  matrix products  25.4 us (4%)
  between operations  15.6 us (2%)
    select_n x62, other arithmetic, sweep_once(): jnp.where((group_counts > sweep_index)[:, None, None], stepped, iterate)  97.1 us
    psum x1, waiting for transfers between devices, on_device(): lax.psum((gram_part, drive_part), ('member', 'space'))  86.6 us
    another operation x16, loops' own time, sweep_group(): return lax.fori_loop(0, jnp.max(group_counts), sweep_once, start_iter)  50.2 us
    all_to_all x1, waiting for transfers between devices, on_device(): lax.all_to_all(jnp.stack(jnp.split(analysis, lax.axis_size('member'), axi...  45.7 us
    all_to_all x1, waiting for transfers between devices, on_device(): lax.all_to_all(final_field, 'member', split_axis=0, concat_axis=0, tiled=...  45.2 us
    all_to_all x1, waiting for transfers between devices, on_device(): lax.all_to_all(state.reshape(local_members, tile_cells), 'member', split_...  44.5 us
    psum x1, blocking collectives, on_device(): lax.psum((gram_part, drive_part), ('member', 'space'))  39.6 us
    slice x17, local copies, waits for them, and re-layouts, relax(): pressure[first_member:first_member + 8]  25.6 us
  transfers between devices with their start and end apart: 8, of which 6 were waited for; matrix products, arithmetic and copies ran while one was open for 5% of the time, Pallas kernels for 0%

profile of v1, /device:TPU:8, one launch (start us, length us, event | category | flops | bytes accessed | tf_op | source)
XLA Modules:
  0.0 654.6 jit_solution(14161417522981812840)
XLA Ops:
  12.4 6.6 %copy.13 = f32[64,4,4096]{2,0,1:T(8,128)} copy(f32[64,4,4096]{2,1,0:T(4,128)} %all_to_all.25) | data formatting | bytes 8388608 | tf_op jit(solution)/shard_map/all_to_all | solution.py:98
  27.7 44.5 %all-to-all-done = f32[64,4,4096]{2,0,1:T(8,128)} async-done(((f32[64,4,4096]{2,0,1:T(8,128)}), f32[64,4,4096]{2,0,1:T(8,128)}, u32[]{:S(2)}, u32[]{:S(2)}) %all-to-all-start) | async-done | bytes 4194336 | tf_op jit(solution)/shard_map/all_to_all | solution.py:98
  74.6 6.2 gather_fusion.1
  100.8 39.6 %psum.15 = f32[256]{0:T(256)S(1)} all-reduce(f32[256]{0:T(256)S(1)} %bitcast.118), channel_id=1, replica_groups=mesh['member'=4,'space'=8] {'member','space'}, use_global_device_ids=true, to_apply=%region_5.6 | all-reduce | flops 256 | bytes 2048 | tf_op jit(solution)/shard_map/psum | solution.py:112
  140.4 86.6 %all-reduce.6.cloned.1.call-done = f32[256,256]{1,0:T(8,128)} async-done(((f32[256,256]{1,0:T(8,128)}), f32[256,256]{1,0:T(8,128)}) %all-reduce.6.cloned.1.call-update) | async-done | bytes 262160 | tf_op jit(solution)/shard_map/psum | solution.py:112
  262.6 45.7 %all-to-all-done.1 = f32[4,64,4096]{2,1,0:T(8,128)} async-done(((f32[4,64,4096]{2,1,0:T(8,128)}), f32[4,64,4096]{2,1,0:T(8,128)}, u32[]{:S(2)}, u32[]{:S(2)}) %all-to-all-start.1) | async-done | bytes 4194336 | tf_op jit(solution)/shard_map/all_to_all | solution.py:130
  308.3 6.9 %copy.19 = f32[64,4,4096]{2,1,0:T(4,128)} copy(f32[64,4,4096]{2,0,1:T(8,128)} %bitcast.16) | data formatting | bytes 8388608 | tf_op jit(solution)/shard_map/reshape | solution.py:129
  363.3 15.0 %fusion.6 = f32[64,16,1024]{2,1,0:T(8,128)S(1)} fusion(f32[64,18,1024]{2,1,0:T(8,128)S(1)} %get-tuple-element.768, f32[64,16,1024]{2,1,0:T(8,128)S(1)} %copy-done.2, f32[64,18,1024]{2,1,0:T(8,128)S(1)} %get-tuple-element.767, f32[65,1,1024]{2,1,0:T(1,128)} %collective-permute-done.1, f32[1,16,1024]{2,1,0:T(8,128)} %bitcast.109, f32[65,1,1024]{2,1,0:T(1,128)} %copy-done.9, ...), kind=kLoop, calls=%fused_computation.58 | loop fusion | flops 28311552 | bytes 34283520 | tf_op jit(solution)/shard_map/add | solution.py:70
  380.3 7.5 %while.168 = (s32[]{:T(128)}, f32[8,16,1024]{2,1,0:T(8,128)}, s32[]{:T(128)}, s32[8]{0:T(128)}, f32[16,1024]{1,0:T(8,128)S(1)}, /*index=5*/f32[8,16,1024]{2,1,0:T(8,128)}, s32[]{:T(128)}) while((s32[]{:T(128)}, f32[8,16,1024]{2,1,0:T(8,128)}, s32[]{:T(128)}, s32[8]{0:T(128)}, f32[16,1024]{1,0:T(8,128)S(1)}, ...), condition=%wide.region_29.30_spmd, body=%wide.region_28.29_spmd.sunk | while | flops 1441802 | bytes 1638537 | solution.py:66
  387.9 9.4 %while.167 = (s32[]{:T(128)}, f32[8,16,1024]{2,1,0:T(8,128)}, s32[]{:T(128)}, s32[8]{0:T(128)S(1)}, f32[16,1024]{1,0:T(8,128)S(1)}, /*index=5*/f32[8,16,1024]{2,1,0:T(8,128)}, s32[]{:T(128)}) while((s32[]{:T(128)}, f32[8,16,1024]{2,1,0:T(8,128)}, s32[]{:T(128)}, s32[8]{0:T(128)S(1)}, f32[16,1024]{1,0:T(8,128)S(1)}, ...), condition=%wide.region_26.27_spmd, body=%wide.region_25.26_spmd.sunk | while | flops 1441802 | bytes 1638537 | solution.py:66
  402.2 7.1 %while.165 = (s32[]{:T(128)}, f32[8,16,1024]{2,1,0:T(8,128)S(1)}, s32[]{:T(128)}, s32[8]{0:T(128)S(1)}, f32[16,1024]{1,0:T(8,128)S(1)}, /*index=5*/f32[8,16,1024]{2,1,0:T(8,128)}, s32[]{:T(128)}) while((s32[]{:T(128)}, f32[8,16,1024]{2,1,0:T(8,128)S(1)}, s32[]{:T(128)}, s32[8]{0:T(128)S(1)}, f32[16,1024]{1,0:T(8,128)S(1)}, ...), condition=%wide.region_20.21_spmd, body=%wide.region_19.20_spmd.sunk | while | flops 1441802 | bytes 1638537 | solution.py:66
  409.3 6.8 %while.164 = (s32[]{:T(128)}, f32[8,16,1024]{2,1,0:T(8,128)S(1)}, s32[]{:T(128)}, s32[8]{0:T(128)S(1)}, f32[16,1024]{1,0:T(8,128)S(1)}, /*index=5*/f32[8,16,1024]{2,1,0:T(8,128)}, s32[]{:T(128)}) while((s32[]{:T(128)}, f32[8,16,1024]{2,1,0:T(8,128)S(1)}, s32[]{:T(128)}, s32[8]{0:T(128)S(1)}, f32[16,1024]{1,0:T(8,128)S(1)}, ...), condition=%wide.region_17.18_spmd, body=%wide.region_16.17_spmd.sunk | while | flops 1441802 | bytes 1638537 | solution.py:66
  416.2 17.4 %while.163 = (s32[]{:T(128)}, f32[8,16,1024]{2,1,0:T(8,128)S(1)}, s32[]{:T(128)}, s32[8]{0:T(128)S(1)}, f32[16,1024]{1,0:T(8,128)S(1)}, /*index=5*/f32[8,16,1024]{2,1,0:T(8,128)}, s32[]{:T(128)}) while((s32[]{:T(128)}, f32[8,16,1024]{2,1,0:T(8,128)S(1)}, s32[]{:T(128)}, s32[8]{0:T(128)S(1)}, f32[16,1024]{1,0:T(8,128)S(1)}, ...), condition=%wide.region_14.15_spmd, body=%wide.region_13.14_spmd.sunk | while | flops 1441802 | bytes 1638537 | solution.py:66
  438.2 17.4 %while.161 = (s32[]{:T(128)}, f32[8,16,1024]{2,1,0:T(8,128)S(1)}, s32[]{:T(128)}, s32[8]{0:T(128)S(1)}, f32[16,1024]{1,0:T(8,128)S(1)}, /*index=5*/f32[8,16,1024]{2,1,0:T(8,128)}, s32[]{:T(128)}) while((s32[]{:T(128)}, f32[8,16,1024]{2,1,0:T(8,128)S(1)}, s32[]{:T(128)}, s32[8]{0:T(128)S(1)}, f32[16,1024]{1,0:T(8,128)S(1)}, ...), condition=%wide.region_8.9_spmd, body=%wide.region_7.8_spmd.sunk | while | flops 1441802 | bytes 1638537 | solution.py:66
  467.0 6.3 collective-permute-done.2
  480.0 10.6 %fusion.18 = f32[64,16,1024]{2,1,0:T(8,128)S(1)} fusion(f32[64,18,1024]{2,1,0:T(8,128)S(1)} %get-tuple-element.770, f32[64,16,1024]{2,1,0:T(8,128)S(1)} %copy-done.8, f32[64,18,1024]{2,1,0:T(8,128)S(1)} %get-tuple-element.769, f32[64,1,1024]{2,1,0:T(1,128)} %collective-permute-done.3, f32[64,1,1024]{2,1,0:T(1,128)} %copy-done.10, f32[16,1024]{1,0:T(8,128)} %param.46, ...), kind=kLoop, calls=%fused_computation.70 | loop fusion | flops 26214400 | bytes 34209792 | tf_op jit(solution)/shard_map/add | solution.py:70
  492.6 7.5 %while.176 = (s32[]{:T(128)}, f32[8,16,1024]{2,1,0:T(8,128)}, s32[]{:T(128)}, s32[8]{0:T(128)}, f32[16,1024]{1,0:T(8,128)S(1)}, /*index=5*/f32[8,16,1024]{2,1,0:T(8,128)}, s32[]{:T(128)}) while((s32[]{:T(128)}, f32[8,16,1024]{2,1,0:T(8,128)}, s32[]{:T(128)}, s32[8]{0:T(128)}, f32[16,1024]{1,0:T(8,128)S(1)}, ...), condition=%wide.region_45.46_spmd, body=%wide.region_44.45_spmd.sunk | while | flops 1441802 | bytes 1638537 | solution.py:66
  500.1 9.4 %while.175 = (s32[]{:T(128)}, f32[8,16,1024]{2,1,0:T(8,128)}, s32[]{:T(128)}, s32[8]{0:T(128)S(1)}, f32[16,1024]{1,0:T(8,128)S(1)}, /*index=5*/f32[8,16,1024]{2,1,0:T(8,128)}, s32[]{:T(128)}) while((s32[]{:T(128)}, f32[8,16,1024]{2,1,0:T(8,128)}, s32[]{:T(128)}, s32[8]{0:T(128)S(1)}, f32[16,1024]{1,0:T(8,128)S(1)}, ...), condition=%wide.region_43.44_spmd, body=%wide.region_42.43_spmd.sunk | while | flops 1441802 | bytes 1638537 | solution.py:66
  514.4 6.9 %while.173 = (s32[]{:T(128)}, f32[8,16,1024]{2,1,0:T(8,128)S(1)}, s32[]{:T(128)}, s32[8]{0:T(128)S(1)}, f32[16,1024]{1,0:T(8,128)S(1)}, /*index=5*/f32[8,16,1024]{2,1,0:T(8,128)}, s32[]{:T(128)}) while((s32[]{:T(128)}, f32[8,16,1024]{2,1,0:T(8,128)S(1)}, s32[]{:T(128)}, s32[8]{0:T(128)S(1)}, f32[16,1024]{1,0:T(8,128)S(1)}, ...), condition=%wide.region_39.40_spmd, body=%wide.region_38.39_spmd.sunk | while | flops 1441802 | bytes 1638537 | solution.py:66
  521.4 6.8 %while.172 = (s32[]{:T(128)}, f32[8,16,1024]{2,1,0:T(8,128)S(1)}, s32[]{:T(128)}, s32[8]{0:T(128)S(1)}, f32[16,1024]{1,0:T(8,128)S(1)}, /*index=5*/f32[8,16,1024]{2,1,0:T(8,128)}, s32[]{:T(128)}) while((s32[]{:T(128)}, f32[8,16,1024]{2,1,0:T(8,128)S(1)}, s32[]{:T(128)}, s32[8]{0:T(128)S(1)}, f32[16,1024]{1,0:T(8,128)S(1)}, ...), condition=%wide.region_37.38_spmd, body=%wide.region_36.37_spmd.sunk | while | flops 1441802 | bytes 1638537 | solution.py:66
  528.2 17.4 %while.171 = (s32[]{:T(128)}, f32[8,16,1024]{2,1,0:T(8,128)S(1)}, s32[]{:T(128)}, s32[8]{0:T(128)S(1)}, f32[16,1024]{1,0:T(8,128)S(1)}, /*index=5*/f32[8,16,1024]{2,1,0:T(8,128)}, s32[]{:T(128)}) while((s32[]{:T(128)}, f32[8,16,1024]{2,1,0:T(8,128)S(1)}, s32[]{:T(128)}, s32[8]{0:T(128)S(1)}, f32[16,1024]{1,0:T(8,128)S(1)}, ...), condition=%wide.region_35.36_spmd, body=%wide.region_34.35_spmd.sunk | while | flops 1441802 | bytes 1638537 | solution.py:66
  550.3 17.4 %while.169 = (s32[]{:T(128)}, f32[8,16,1024]{2,1,0:T(8,128)S(1)}, s32[]{:T(128)}, s32[8]{0:T(128)S(1)}, f32[16,1024]{1,0:T(8,128)S(1)}, /*index=5*/f32[8,16,1024]{2,1,0:T(8,128)}, s32[]{:T(128)}) while((s32[]{:T(128)}, f32[8,16,1024]{2,1,0:T(8,128)S(1)}, s32[]{:T(128)}, s32[8]{0:T(128)S(1)}, f32[16,1024]{1,0:T(8,128)S(1)}, ...), condition=%wide.region_31.32_spmd, body=%wide.region_30.31_spmd.sunk | while | flops 1441802 | bytes 1638537 | solution.py:66
  587.5 45.2 %all-to-all-done.2 = f32[4,16,16384]{2,1,0:T(8,128)} async-done(((f32[4,16,16384]{2,1,0:T(8,128)}), f32[4,16,16384]{2,1,0:T(8,128)}, u32[]{:S(2)}, u32[]{:S(2)}) %all-to-all-start.2) | async-done | bytes 4194336 | tf_op jit(solution)/shard_map/all_to_all | solution.py:143
  632.7 7.7 %gather_fusion.4 = f32[64,16384]{1,0:T(8,128)} fusion(f32[64,16384]{1,0:T(8,128)} %bitcast.19, s32[1024]{0:T(1024)S(1)} %pad_clamp_fusion), kind=kCustom, calls=%fused_computation.4 | custom fusion | bytes 8388864 | tf_op jit(solution)/shard_map/jit(_take)/gather | solution.py:148
  (319 shorter events, 286.8 us)
Async XLA Ops:
  19.0 8.7 %copy-start.14 = (s32[1024]{0:T(1024)S(1)}, s32[1024]{0:T(1024)}, u32[]{:S(2)}) copy-start(s32[1024]{0:T(1024)} %param.41) | copy-start | bytes 12292
  19.0 53.2 %all-to-all-start = ((f32[64,4,4096]{2,0,1:T(8,128)}), f32[64,4,4096]{2,0,1:T(8,128)}, u32[]{:S(2)}, u32[]{:S(2)}) async-start(f32[64,4,4096]{2,0,1:T(8,128)} %copy.13), calls=%async_computation | async-start | bytes 8388608 | tf_op jit(solution)/shard_map/all_to_all | solution.py:98
  24.0 203.0 %all-reduce.6.cloned.1.call-start = ((), (), s32[]{:S(2)}) async-start(), calls=%async_computation.3 | async-start | bytes 524288 | tf_op jit(solution)/shard_map/psum | solution.py:112
  27.3 44.8 %copy-start.13 = (s32[4,16,4]{2,1,0:T(8,128)}, s32[4,16,4]{2,1,0:T(8,128)S(1)}, u32[]{:S(2)}) copy-start(s32[4,16,4]{2,1,0:T(8,128)S(1)} %reshape.164) | copy-start | bytes 3076
  255.2 53.1 %all-to-all-start.1 = ((f32[4,64,4096]{2,1,0:T(8,128)}), f32[4,64,4096]{2,1,0:T(8,128)}, u32[]{:S(2)}, u32[]{:S(2)}) async-start(f32[4,64,4096]{2,1,0:T(8,128)} %pad_maximum_fusion.10), calls=%async_computation.1 | async-start | bytes 8388608 | tf_op jit(solution)/shard_map/all_to_all | solution.py:130
  324.6 32.6 %collective-permute-start = (f32[65,1,1024]{2,1,0:T(1,128)}, f32[65,1,1024]{2,1,0:T(1,128)S(1)}, u32[]{:S(2)}, u32[]{:S(2)}) collective-permute-start(f32[65,1,1024]{2,1,0:T(1,128)} %get-tuple-element.771), channel_id=1, source_target_pairs={{0,1},{1,2},{2,3},{3,4},{4,5},{5,6},{6,7},{8,9},{9,10},{10,11},{11... | collective-permute-start | bytes 798728 | tf_op jit(solution)/shard_map/ppermute | solution.py:19
  328.0 29.2 %collective-permute-start.1 = (f32[65,1,1024]{2,1,0:T(1,128)}, f32[65,1,1024]{2,1,0:T(1,128)}, u32[]{:S(2)}, u32[]{:S(2)}) collective-permute-start(f32[65,1,1024]{2,1,0:T(1,128)} %get-tuple-element.772), channel_id=1, source_target_pairs={{1,0},{2,1},{3,2},{4,3},{5,4},{6,5},{7,6},{9,8},{10,9},{11,10},{12... | collective-permute-start | bytes 798728 | tf_op jit(solution)/shard_map/ppermute | solution.py:20
  357.2 6.1 copy-start.9
  380.3 7.6 %copy-start.27 = (s32[8]{0:T(128)S(1)}, s32[8]{0:T(128)}, u32[]{:S(2)}) copy-start(s32[8]{0:T(128)} %get-tuple-element.1718) | copy-start | bytes 100
  387.9 9.4 %copy-start.25 = (s32[8]{0:T(128)S(1)}, s32[8]{0:T(128)}, u32[]{:S(2)}) copy-start(s32[8]{0:T(128)} %get-tuple-element.1697) | copy-start | bytes 100
  402.1 7.2 %copy-start.21 = (s32[8]{0:T(128)S(1)}, s32[8]{0:T(128)}, u32[]{:S(2)}) copy-start(s32[8]{0:T(128)} %get-tuple-element.1655) | copy-start | bytes 100
  409.3 6.9 %copy-start.19 = (s32[8]{0:T(128)S(1)}, s32[8]{0:T(128)}, u32[]{:S(2)}) copy-start(s32[8]{0:T(128)} %get-tuple-element.1634) | copy-start | bytes 100
  416.2 17.5 %copy-start.17 = (s32[8]{0:T(128)S(1)}, s32[8]{0:T(128)}, u32[]{:S(2)}) copy-start(s32[8]{0:T(128)} %get-tuple-element.1613) | copy-start | bytes 100
  460.2 13.1 %collective-permute-start.2 = (f32[64,1,1024]{2,1,0:T(1,128)}, f32[64,1,1024]{2,1,0:T(1,128)S(1)}, u32[]{:S(2)}, u32[]{:S(2)}) collective-permute-start(f32[64,1,1024]{2,1,0:T(1,128)} %get-tuple-element.781), channel_id=1, source_target_pairs={{0,1},{1,2},{2,3},{3,4},{4,5},{5,6},{6,7},{8,9},{9,10},{10,11},{11... | collective-permute-start | bytes 786440 | tf_op jit(solution)/shard_map/ppermute | solution.py:19
  462.7 13.4 %collective-permute-start.3 = (f32[64,1,1024]{2,1,0:T(1,128)}, f32[64,1,1024]{2,1,0:T(1,128)}, u32[]{:S(2)}, u32[]{:S(2)}) collective-permute-start(f32[64,1,1024]{2,1,0:T(1,128)} %get-tuple-element.782), channel_id=1, source_target_pairs={{1,0},{2,1},{3,2},{4,3},{5,4},{6,5},{7,6},{9,8},{10,9},{11,10},{12... | collective-permute-start | bytes 786440 | tf_op jit(solution)/shard_map/ppermute | solution.py:20
  467.0 13.0 %copy-start.8 = (f32[64,16,1024]{2,1,0:T(8,128)S(1)}, f32[64,16,1024]{2,1,0:T(8,128)}, u32[]{:S(2)}) copy-start(f32[64,16,1024]{2,1,0:T(8,128)} %copy-done.7) | copy-start | bytes 12582916
  473.3 6.6 %copy-start.10 = (f32[64,1,1024]{2,1,0:T(1,128)}, f32[64,1,1024]{2,1,0:T(1,128)S(1)}, u32[]{:S(2)}) copy-start(f32[64,1,1024]{2,1,0:T(1,128)S(1)} %collective-permute-done.2) | copy-start | bytes 786436
  492.6 7.6 %copy-start.28 = (s32[8]{0:T(128)S(1)}, s32[8]{0:T(128)}, u32[]{:S(2)}) copy-start(s32[8]{0:T(128)} %get-tuple-element.1718) | copy-start | bytes 100
  500.1 9.4 %copy-start.26 = (s32[8]{0:T(128)S(1)}, s32[8]{0:T(128)}, u32[]{:S(2)}) copy-start(s32[8]{0:T(128)} %get-tuple-element.1697) | copy-start | bytes 100
  514.4 7.0 %copy-start.22 = (s32[8]{0:T(128)S(1)}, s32[8]{0:T(128)}, u32[]{:S(2)}) copy-start(s32[8]{0:T(128)} %get-tuple-element.1655) | copy-start | bytes 100
  521.4 6.9 %copy-start.20 = (s32[8]{0:T(128)S(1)}, s32[8]{0:T(128)}, u32[]{:S(2)}) copy-start(s32[8]{0:T(128)} %get-tuple-element.1634) | copy-start | bytes 100
  528.2 17.5 %copy-start.18 = (s32[8]{0:T(128)S(1)}, s32[8]{0:T(128)}, u32[]{:S(2)}) copy-start(s32[8]{0:T(128)} %get-tuple-element.1613) | copy-start | bytes 100
  567.7 5.9 copy-start.6
  579.4 53.3 %all-to-all-start.2 = ((f32[4,16,16384]{2,1,0:T(8,128)}), f32[4,16,16384]{2,1,0:T(8,128)}, u32[]{:S(2)}, u32[]{:S(2)}) async-start(f32[4,16,16384]{2,1,0:T(8,128)} %all_to_all.30), calls=%async_computation.2 | async-start | bytes 8388608 | tf_op jit(solution)/shard_map/all_to_all | solution.py:143
  (13 other events, 51.3 us)
Sparse Core Ops, SparseCore 0:
  100.1 126.7 all-reduce.5
